TPU v7x, 32 devices: a whole 2x2x4 slice. The times are simulated.
32 devices in a mesh: wide: 8 (over z, y), narrow: 4 (over x, core).
Axes of the slice: x: 2, y: 2, z: 4, core: 2. Of those that a mesh axis runs over, the one named last changes fastest.
Arguments:
- layer_in: bfloat16 [8, 512, 1536], P('wide', 'narrow'), may hold values from -6 to 6
- lengths: int32 [8, 8], P('wide'), may hold values from 1 to 256, 512 in all within a row
- w_qkv: bfloat16 [1536, 2048], P(('wide', 'narrow')), may hold values from -0.15625 to 0.15625
- b_qkv: bfloat16 [2048], P(('wide', 'narrow')), may hold values from -3 to 3
- w_out: bfloat16 [1536, 1536], P(None, ('wide', 'narrow')), may hold values from -0.625 to 0.625
- norm1_gain: bfloat16 [1536], P(('wide', 'narrow')), may hold values from 0.099609375 to 1.8984375
- norm2_gain: bfloat16 [1536], P(('wide', 'narrow')), may hold values from 0.099609375 to 1.8984375
- w_gate: bfloat16 [1536, 8960], P('wide', 'narrow'), may hold values from -0.15625 to 0.15625
- w_up: bfloat16 [1536, 8960], P('wide', 'narrow'), may hold values from -0.15625 to 0.15625
- w_down: bfloat16 [8960, 1536], P('narrow', 'wide'), may hold values from -0.0625 to 0.0625
- grad_out: bfloat16 [8, 512, 1536], P('wide', 'narrow'), may hold values from -6 to 6
Outputs:
- layer_out: bfloat16 [8, 512, 1536], P('wide', 'narrow')
- grad_in: float32 [8, 512, 1536], P('wide', 'narrow')
- grad_w_qkv: float32 [1536, 2048], P(('wide', 'narrow'))
- grad_b_qkv: float32 [2048], P(('wide', 'narrow'))
- grad_w_out: float32 [1536, 1536], P(None, ('wide', 'narrow'))
- grad_norm1: float32 [1536], P(('wide', 'narrow'))
- grad_norm2: float32 [1536], P(('wide', 'narrow'))
- grad_w_gate: float32 [1536, 8960], P('wide', 'narrow')
- grad_w_up: float32 [1536, 8960], P('wide', 'narrow')
- grad_w_down: float32 [8960, 1536], P('narrow', 'wide')
Inputs may be any that keep to these rules, and one draw needn't show every extreme that they name: In each pack the 8 lengths sum to 512, and one of them is 256.
All inputs are finite; a program needn't handle non-finite values.
Results may differ from a plain program's by a relative error of at most 0.02.
Values may be sent and summed in bfloat16 or wider, within the bound.
A program may use at most 192 MiB of HBM per device.

v0:
```python
import math
import jax
import jax.numpy as jnp
from jax import lax
from jax.sharding import PartitionSpec as P

QUERY_HEADS = 12
KEY_VALUE_HEADS = 2
HEAD_WIDTH = 128
EPSILON = 1e-06
ROPE_BASE = 10000.0
NEGATIVE_BIG = -1e30
HIGHEST = lax.Precision.HIGHEST


def rms_scale(value_rows, gain):
    return (
        value_rows
        * lax.rsqrt(jnp.mean(value_rows * value_rows, axis=-1, keepdims=True) + EPSILON)
        * gain
    )


def apply_rotation(value_rows, token_position):
    half_dim = value_rows.shape[-1] // 2
    freq = jnp.exp(
        jnp.arange(half_dim, dtype=jnp.float32)
        * (-2.0 * math.log(ROPE_BASE) / value_rows.shape[-1])
    )
    angle = token_position[:, None] * freq[None, :]
    cosine = jnp.cos(angle)[:, None, :]
    sine = jnp.sin(angle)[:, None, :]
    leading = value_rows[..., :half_dim]
    trailing = value_rows[..., half_dim:]
    return jnp.concatenate(
        [leading * cosine - trailing * sine, trailing * cosine + leading * sine], axis=-1
    )


def doc_layout(index, doc_lengths):
    ends = jnp.cumsum(doc_lengths)
    starts = ends - doc_lengths
    document_index = jnp.sum((index[:, None] >= ends[None, :]).astype(jnp.int32), axis=1)
    onehot = (
        document_index[:, None] == jnp.arange(doc_lengths.shape[0], dtype=jnp.int32)[None, :]
    ).astype(jnp.int32)
    token_position = index - jnp.sum(onehot * starts[None, :], axis=1)
    return (document_index, token_position.astype(jnp.float32))


def contract_rows(left, right):
    return lax.dot_general(
        left, right, (((0,), (0,)), ((), ())), preferred_element_type=jnp.float32
    )


def times_transposed(left, right):
    return lax.dot_general(
        left, right, (((1,), (1,)), ((), ())), preferred_element_type=jnp.float32
    )


def shards(
    layer_in, lengths, w_qkv, b_qkv, w_out, norm1_gain, norm2_gain, w_gate, w_up, w_down, grad_out
):
    hidden_in = layer_in[0].astype(jnp.float32)
    rows_per_shard = hidden_in.shape[0]
    narrow_count = lax.axis_size("narrow")
    first_row = lax.axis_index("narrow") * rows_per_shard
    pack_rows = rows_per_shard * narrow_count
    query_group = QUERY_HEADS // KEY_VALUE_HEADS
    query_total_width = QUERY_HEADS * HEAD_WIDTH
    key_total_width = KEY_VALUE_HEADS * HEAD_WIDTH
    scale = HEAD_WIDTH ** (-0.5)
    doc_lengths = lengths[0]
    local_index = first_row + jnp.arange(rows_per_shard, dtype=jnp.int32)
    local_doc, local_pos = doc_layout(local_index, doc_lengths)
    key_index = jnp.arange(pack_rows, dtype=jnp.int32)
    key_doc = doc_layout(key_index, doc_lengths)[0]
    wqkv_full, bias_full, wout_full, gain_one, gain_two = (
        lax.all_gather(w_qkv, ("wide", "narrow"), axis=0, tiled=True),
        lax.all_gather(b_qkv, ("wide", "narrow"), axis=0, tiled=True),
        lax.all_gather(w_out, ("wide", "narrow"), axis=1, tiled=True),
        lax.all_gather(norm1_gain, ("wide", "narrow"), axis=0, tiled=True),
        lax.all_gather(norm2_gain, ("wide", "narrow"), axis=0, tiled=True),
    )
    wgate_full, wup_full, wdown_full = (
        lax.all_gather(w_gate, "wide", axis=0, tiled=True),
        lax.all_gather(w_up, "wide", axis=0, tiled=True),
        lax.all_gather(w_down, "wide", axis=1, tiled=True),
    )
    gain_one = gain_one.astype(jnp.float32)
    gain_two = gain_two.astype(jnp.float32)
    normed_one = rms_scale(hidden_in, gain_one).astype(jnp.bfloat16)
    unrotated_projection = jnp.dot(
        normed_one, wqkv_full, preferred_element_type=jnp.float32
    ) + bias_full.astype(jnp.float32)
    pre_query = unrotated_projection[:, :query_total_width].reshape(
        rows_per_shard, QUERY_HEADS, HEAD_WIDTH
    )
    unrotated_key = unrotated_projection[
        :, query_total_width : query_total_width + key_total_width
    ].reshape(rows_per_shard, KEY_VALUE_HEADS, HEAD_WIDTH)

    def rotate_local(value_rows):
        return apply_rotation(value_rows, local_pos)

    rotated_query, query_back = jax.vjp(rotate_local, pre_query)
    key_rot, key_backward = jax.vjp(rotate_local, unrotated_key)
    query_rows = rotated_query.astype(jnp.bfloat16).reshape(
        rows_per_shard, KEY_VALUE_HEADS, query_group, HEAD_WIDTH
    )
    key_local = key_rot.reshape(rows_per_shard, key_total_width).astype(jnp.bfloat16)
    value_local = unrotated_projection[:, query_total_width + key_total_width :].astype(
        jnp.bfloat16
    )
    every_key_row, every_value_row = (
        lax.all_gather(key_local, "narrow", axis=0, tiled=True),
        lax.all_gather(value_local, "narrow", axis=0, tiled=True),
    )
    rows_per_block = min(512, pack_rows)
    count_of_blocks = pack_rows // rows_per_block
    blocked_keys = every_key_row.reshape(
        count_of_blocks, rows_per_block, KEY_VALUE_HEADS, HEAD_WIDTH
    )
    blocked_values = every_value_row.reshape(
        count_of_blocks, rows_per_block, KEY_VALUE_HEADS, HEAD_WIDTH
    )
    doc_blocks = key_doc.reshape(count_of_blocks, rows_per_block)
    index_blocks = key_index.reshape(count_of_blocks, rows_per_block)
    input_per_block = (blocked_keys, blocked_values, doc_blocks, index_blocks)

    def block_scores(key_block, doc_block, index_block):
        scores = (
            jnp.einsum("tkgd,skd->kgts", query_rows, key_block, preferred_element_type=jnp.float32)
            * scale
        )
        allowed = (local_doc[:, None] == doc_block[None, :]) & (
            index_block[None, :] <= local_index[:, None]
        )
        return (jnp.where(allowed, scores, NEGATIVE_BIG), allowed)

    def total_block(carry, inputs):
        running_max, running_sum = carry
        key_block, value_block, doc_block, index_block = inputs
        masked, allowed = block_scores(key_block, doc_block, index_block)
        new_max = jnp.maximum(running_max, jnp.max(masked, axis=-1))
        probs = jnp.where(allowed, jnp.exp(masked - new_max[..., None]), 0.0)
        running_sum = running_sum * jnp.exp(running_max - new_max) + jnp.sum(probs, axis=-1)
        return ((new_max, running_sum), None)

    start_carry = (
        jnp.full((KEY_VALUE_HEADS, query_group, rows_per_shard), NEGATIVE_BIG, jnp.float32),
        jnp.zeros((KEY_VALUE_HEADS, query_group, rows_per_shard), jnp.float32),
    )
    (final_max, final_sum), _ = lax.scan(total_block, start_carry, input_per_block)
    log_total = final_max + jnp.log(final_sum)

    def block_probs(key_block, doc_block, index_block):
        masked, allowed = block_scores(key_block, doc_block, index_block)
        return jnp.where(allowed, jnp.exp(masked - log_total[..., None]), 0.0)

    def block_forward_pass(weighted, inputs):
        key_block, value_block, doc_block, index_block = inputs
        probs_low = block_probs(key_block, doc_block, index_block).astype(jnp.bfloat16)
        weighted = weighted + jnp.einsum(
            "kgts,skd->kgtd", probs_low, value_block, preferred_element_type=jnp.float32
        )
        return (weighted, None)

    attn_heads, _ = lax.scan(
        block_forward_pass,
        jnp.zeros((KEY_VALUE_HEADS, query_group, rows_per_shard, HEAD_WIDTH), jnp.float32),
        input_per_block,
    )
    attn_low = (
        attn_heads.transpose(2, 0, 1, 3)
        .reshape(rows_per_shard, query_total_width)
        .astype(jnp.bfloat16)
    )
    middle = hidden_in + jnp.dot(attn_low, wout_full, preferred_element_type=jnp.float32)
    normed_two = rms_scale(middle, gain_two).astype(jnp.bfloat16)
    pack_normed = lax.all_gather(normed_two, "narrow", axis=0, tiled=True)
    gate = jnp.dot(pack_normed, wgate_full, preferred_element_type=jnp.float32)
    up_part = jnp.dot(pack_normed, wup_full, preferred_element_type=jnp.float32)
    sigmoid_gate = jax.nn.sigmoid(gate)
    activated = gate * sigmoid_gate
    hidden_act = (activated * up_part).astype(jnp.bfloat16)
    mixed = lax.psum_scatter(
        jnp.dot(hidden_act, wdown_full, preferred_element_type=jnp.float32).astype(jnp.bfloat16),
        "narrow",
        scatter_dimension=0,
        tiled=True,
    ).astype(jnp.float32)
    layer_out = (middle + mixed).astype(jnp.bfloat16)
    wgate_back, wup_back, wdown_back = (
        lax.all_gather(w_gate, "wide", axis=0, tiled=True),
        lax.all_gather(w_up, "wide", axis=0, tiled=True),
        lax.all_gather(w_down, "wide", axis=1, tiled=True),
    )
    cotangent = grad_out[0]
    pack_cotangent = lax.all_gather(cotangent, "narrow", axis=0, tiled=True)
    grad_hidden = times_transposed(pack_cotangent, wdown_back)
    grad_wdown = contract_rows(hidden_act, pack_cotangent)
    grad_gate = (grad_hidden * up_part * sigmoid_gate * (1.0 + gate * (1.0 - sigmoid_gate))).astype(
        jnp.bfloat16
    )
    grad_up = (grad_hidden * activated).astype(jnp.bfloat16)
    grad_wgate = contract_rows(pack_normed, grad_gate)
    grad_wup = contract_rows(pack_normed, grad_up)
    grad_normed_two = lax.psum_scatter(
        (times_transposed(grad_gate, wgate_back) + times_transposed(grad_up, wup_back)).astype(
            jnp.bfloat16
        ),
        "narrow",
        scatter_dimension=0,
        tiled=True,
    ).astype(jnp.float32)
    norm_two_back = jax.vjp(rms_scale, middle, gain_two)[1]
    grad_middle_norm, grad_gain_two = norm_two_back(grad_normed_two)
    grad_middle = cotangent.astype(jnp.float32) + grad_middle_norm
    grad_attn_proj = grad_middle.astype(jnp.bfloat16)
    grad_wout = contract_rows(attn_low, grad_attn_proj)
    attention_gradient = times_transposed(grad_attn_proj, wout_full).astype(jnp.bfloat16)
    head_gradients = attention_gradient.reshape(
        rows_per_shard, KEY_VALUE_HEADS, query_group, HEAD_WIDTH
    )
    delta = jnp.einsum(
        "tkgd,kgtd->kgt", head_gradients.astype(jnp.float32), attn_heads, precision=HIGHEST
    )

    def block_backward_pass(grad_query, inputs):
        key_block, value_block, doc_block, index_block = inputs
        probs = block_probs(key_block, doc_block, index_block)
        grad_probs = jnp.einsum(
            "tkgd,skd->kgts", head_gradients, value_block, preferred_element_type=jnp.float32
        )
        grad_scores = (probs * (grad_probs - delta[..., None])).astype(jnp.bfloat16)
        grad_query = (
            grad_query
            + jnp.einsum(
                "kgts,skd->tkgd", grad_scores, key_block, preferred_element_type=jnp.float32
            )
            * scale
        )
        grad_key = (
            jnp.einsum(
                "kgts,tkgd->skd", grad_scores, query_rows, preferred_element_type=jnp.float32
            )
            * scale
        )
        grad_value = jnp.einsum(
            "kgts,tkgd->skd",
            probs.astype(jnp.bfloat16),
            head_gradients,
            preferred_element_type=jnp.float32,
        )
        return (grad_query, (grad_key, grad_value))

    grad_query, (grad_key_blocks, grad_value_blocks) = lax.scan(
        block_backward_pass,
        jnp.zeros((rows_per_shard, KEY_VALUE_HEADS, query_group, HEAD_WIDTH), jnp.float32),
        input_per_block,
    )
    local_key_gradients, grad_values_local = (
        lax.psum_scatter(
            grad_key_blocks.reshape(pack_rows, key_total_width).astype(jnp.bfloat16),
            "narrow",
            scatter_dimension=0,
            tiled=True,
        ).astype(jnp.float32),
        lax.psum_scatter(
            grad_value_blocks.reshape(pack_rows, key_total_width).astype(jnp.bfloat16),
            "narrow",
            scatter_dimension=0,
            tiled=True,
        ).astype(jnp.float32),
    )
    grad_pre_query = query_back(grad_query.reshape(rows_per_shard, QUERY_HEADS, HEAD_WIDTH))[0]
    unrotated_key_gradient = key_backward(
        local_key_gradients.reshape(rows_per_shard, KEY_VALUE_HEADS, HEAD_WIDTH)
    )[0]
    grad_pre = jnp.concatenate(
        [
            grad_pre_query.reshape(rows_per_shard, query_total_width),
            unrotated_key_gradient.reshape(rows_per_shard, key_total_width),
            grad_values_local,
        ],
        axis=1,
    ).astype(jnp.bfloat16)
    grad_bias = jnp.sum(grad_pre.astype(jnp.float32), axis=0)
    grad_wqkv = contract_rows(normed_one, grad_pre)
    grad_normed_one = times_transposed(grad_pre, wqkv_full)
    norm_one_back = jax.vjp(rms_scale, hidden_in, gain_one)[1]
    grad_input_norm, grad_gain_one = norm_one_back(grad_normed_one)
    grad_input = grad_middle + grad_input_norm
    sum_wqkv, sum_bias, sum_wout, sum_gain_one, sum_gain_two = (
        lax.psum_scatter(grad_wqkv, ("wide", "narrow"), scatter_dimension=0, tiled=True),
        lax.psum_scatter(grad_bias, ("wide", "narrow"), scatter_dimension=0, tiled=True),
        lax.psum_scatter(grad_wout, ("wide", "narrow"), scatter_dimension=1, tiled=True),
        lax.psum_scatter(grad_gain_one, ("wide", "narrow"), scatter_dimension=0, tiled=True),
        lax.psum_scatter(grad_gain_two, ("wide", "narrow"), scatter_dimension=0, tiled=True),
    )
    sum_wgate, sum_wup, sum_wdown = (
        lax.psum_scatter(
            grad_wgate.astype(jnp.bfloat16), "wide", scatter_dimension=0, tiled=True
        ).astype(jnp.float32),
        lax.psum_scatter(
            grad_wup.astype(jnp.bfloat16), "wide", scatter_dimension=0, tiled=True
        ).astype(jnp.float32),
        lax.psum_scatter(
            grad_wdown.astype(jnp.bfloat16), "wide", scatter_dimension=1, tiled=True
        ).astype(jnp.float32),
    )
    return (
        layer_out[None],
        grad_input[None],
        sum_wqkv,
        sum_bias,
        sum_wout,
        sum_gain_one,
        sum_gain_two,
        sum_wgate,
        sum_wup,
        sum_wdown,
    )


def solution(mesh):
    placed = (
        P("wide", "narrow", None),
        P("wide", None),
        P(("wide", "narrow"), None),
        P(("wide", "narrow")),
        P(None, ("wide", "narrow")),
        P(("wide", "narrow")),
        P(("wide", "narrow")),
        P("wide", "narrow"),
        P("wide", "narrow"),
        P("narrow", "wide"),
        P("wide", "narrow", None),
    )
    return jax.shard_map(
        shards,
        mesh=mesh,
        in_specs=placed,
        out_specs=(
            P("wide", "narrow", None),
            P("wide", "narrow", None),
            P(("wide", "narrow"), None),
            P(("wide", "narrow")),
            P(None, ("wide", "narrow")),
            P(("wide", "narrow")),
            P(("wide", "narrow")),
            P("wide", "narrow"),
            P("wide", "narrow"),
            P("narrow", "wide"),
        ),
        check_vma=False,
    )
```

profile of v0, /device:TPU:0, one launch (start us, length us, event | category | flops | bytes accessed | tf_op | source)
XLA Modules:
  0.0 1367.8 jit_solution(4092313823965801265)
XLA Ops:
  9.5 0.9 dynamic-update-slice
  12.0 42.5 %all-reduce.11 = (bf16[2048]{0:T(1024)(128)(2,1)S(1)}, bf16[1536]{0:T(1024)(128)(2,1)S(1)}, bf16[1536]{0:T(1024)(128)(2,1)S(1)}) all-reduce(bf16[2048]{0:T(1024)(128)(2,1)S(1)} %dynamic-update-slice.1, bf16[1536]{0:T(1024)(128)(2,1)S(1)} %dynamic-update-slice, ...), channel_id=1, replica_groups=mesh['wide'=8,'narrow'=4] {'wide','narrow'}, use_global_device_ids=true, to_apply=%add.5 | all-reduce | flops 5120 | bytes 20480
  56.8 1.2 fusion.23
  58.7 24.4 %all-gather.9.cloned.1.call-done = bf16[1536,2048]{1,0:T(8,128)(2,1)} async-done(((bf16[48,2048]{1,0:T(8,128)(2,1)}), bf16[1536,2048]{1,0:T(8,128)(2,1)}) %all-gather.9.cloned.1.call-update) | async-done | bytes 6291472 | tf_op jit(solution)/shard_map/all_gather | solution.py:81
  83.1 4.0 convolution_add_fusion.2
  88.5 0.9 copy.116
  89.4 5.8 all_gather.43
  95.2 0.9 copy.132
  96.1 5.9 all_gather.42
  102.0 1.9 fusion.5
  104.0 1.6 select_reduce_fusion
  106.2 1.9 fusion.46
  108.1 40.1 %all-gather.11.cloned.1.call-done = bf16[1536,1536]{0,1:T(8,128)(2,1)} async-done(((bf16[1536,48]{0,1:T(8,128)(2,1)}), bf16[1536,1536]{0,1:T(8,128)(2,1)}) %all-gather.11.cloned.1.call-update) | async-done | bytes 4718608 | tf_op jit(solution)/shard_map/all_gather | solution.py:83
  148.2 4.2 multiply_reduce_fusion
  153.4 0.9 multiply_convert_fusion.3
  156.5 100.5 %all-gather.15.cloned.1.call-done = bf16[1536,2240]{1,0:T(8,128)(2,1)} async-done(((bf16[192,2240]{1,0:T(8,128)(2,1)}), bf16[1536,2240]{1,0:T(8,128)(2,1)}) %all-gather.15.cloned.1.call-update) | async-done | bytes 6881296 | tf_op jit(solution)/shard_map/all_gather | solution.py:88
  257.0 19.8 %all-gather.13.cloned.1.call-done = bf16[512,1536]{1,0:T(8,128)(2,1)} async-done(((bf16[128,1536]{1,0:T(8,128)(2,1)}), bf16[512,1536]{1,0:T(8,128)(2,1)}) %all-gather.13.cloned.1.call-update) | async-done | bytes 1572880 | tf_op jit(solution)/shard_map/all_gather | solution.py:183
  276.8 9.5 fusion.47
  286.3 100.9 %all-gather.17.cloned.1.call-done = bf16[1536,2240]{1,0:T(8,128)(2,1)} async-done(((bf16[192,2240]{1,0:T(8,128)(2,1)}), bf16[1536,2240]{1,0:T(8,128)(2,1)}) %all-gather.17.cloned.1.call-update) | async-done | bytes 6881296 | tf_op jit(solution)/shard_map/all_gather | solution.py:89
  387.2 9.3 fusion.48
  396.5 9.9 all-gather.21.cloned.1.call-done
  406.5 110.5 %all-gather.19.cloned.1.call-done = bf16[2240,1536]{0,1:T(8,128)(2,1)} async-done(((bf16[2240,192]{0,1:T(8,128)(2,1)}), bf16[2240,1536]{0,1:T(8,128)(2,1)}) %all-gather.19.cloned.1.call-update) | async-done | bytes 6881296 | tf_op jit(solution)/shard_map/all_gather | solution.py:90
  517.0 13.3 multiply_convert_fusion
  530.3 7.8 fusion.49
  538.2 5.0 fusion.3
  543.3 8.8 convolution_convert_fusion.3
  552.5 17.1 %reduce-scatter.16.cloned.1.call-done = bf16[128,1536]{1,0:T(8,128)(2,1)} async-done(((bf16[512,1536]{1,0:T(8,128)(2,1)}), bf16[128,1536]{1,0:T(8,128)(2,1)}) %reduce-scatter.16.cloned.1.call-update) | async-done | bytes 393232 | tf_op jit(solution)/shard_map/reduce_scatter | solution.py:211
  569.6 2.1 fusion.19
  571.7 1.2 multiply_multiply_fusion.1
  572.8 27.9 %reduce-scatter.14.cloned.1.call-done = bf16[128,1536]{1,0:T(8,128)(2,1)} async-done(((bf16[512,1536]{1,0:T(8,128)(2,1)}), bf16[128,1536]{1,0:T(8,128)(2,1)}) %reduce-scatter.14.cloned.1.call-update) | async-done | bytes 393232 | tf_op jit(solution)/shard_map/reduce_scatter | solution.py:189
  600.8 2.5 fusion.20
  603.3 0.9 copy-done.1
  604.2 3.9 convolution_convert_fusion.4
  608.1 1.9 copy.120
  610.0 1.3 fusion.25
  611.4 2.3 fusion.2
  613.7 1.1 copy-done.4
  614.8 1.5 fusion.10
  616.4 1.8 copy.155
  618.2 2.6 fusion.11
  620.8 1.8 copy.157
  622.7 8.9 convolution_convert_fusion.2
  631.7 1.3 copy-done.32
  633.1 7.6 convolution_convert_fusion.1
  640.9 1.2 copy-done.33
  642.1 7.5 convolution_convert_fusion
  649.7 1.1 copy-done.2
  650.8 5.0 fusion.28
  656.0 1.3 copy-done.5
  657.9 0.9 copy.156
  659.4 2.1 reduce-scatter.30.cloned.1.call-done
  661.5 0.9 copy.158
  662.5 6.4 fusion.31
  669.2 5.1 fusion.17
  674.3 43.1 %all-reduce.10 = (f32[2048]{0:T(1024)S(1)}, f32[1536]{0:T(1024)S(1)}, f32[1536]{0:T(1024)S(1)}) all-reduce(f32[2048]{0:T(1024)S(1)} %convert_reduce_fusion, f32[1536]{0:T(1024)S(1)} %get-tuple-element.83, f32[1536]{0:T(1024)S(1)} %copy-done.22), channel_id=8, replica_groups=mesh['wide'=8,'narrow'=4] {'wide','narrow'}, use_global_device_ids=true, to_apply=%region_16.17.clone | all-reduce | flops 5120 | bytes 40960
  719.2 1.1 fusion.22
  720.3 75.0 %reduce-scatter.22.cloned.1.call-done = bf16[192,2240]{1,0:T(8,128)(2,1)} async-done(((bf16[1536,2240]{1,0:T(8,128)(2,1)}), bf16[192,2240]{1,0:T(8,128)(2,1)}) %reduce-scatter.22.cloned.1.call-update) | async-done | bytes 860176 | tf_op jit(solution)/shard_map/reduce_scatter | solution.py:305
  795.3 2.5 convert_element_type.172
  797.8 129.5 %reduce-scatter.24.cloned.1.call-done = bf16[192,2240]{1,0:T(8,128)(2,1)} async-done(((bf16[1536,2240]{1,0:T(8,128)(2,1)}), bf16[192,2240]{1,0:T(8,128)(2,1)}) %reduce-scatter.24.cloned.1.call-update) | async-done | bytes 860176 | tf_op jit(solution)/shard_map/reduce_scatter | solution.py:308
  927.3 2.5 convert_element_type.174
  929.8 129.4 %reduce-scatter.26.cloned.1.call-done = bf16[2240,192]{0,1:T(8,128)(2,1)} async-done(((bf16[2240,1536]{0,1:T(8,128)(2,1)}), bf16[2240,192]{0,1:T(8,128)(2,1)}) %reduce-scatter.26.cloned.1.call-update) | async-done | bytes 860176 | tf_op jit(solution)/shard_map/reduce_scatter | solution.py:311
  1059.1 2.5 convert_element_type.176
  1061.6 139.1 %reduce-scatter.20.cloned.1.call-done = f32[1536,48]{0,1:T(8,128)} async-done(((f32[1536,1536]{0,1:T(8,128)}), f32[1536,48]{0,1:T(8,128)}) %reduce-scatter.20.cloned.1.call-update) | async-done | bytes 294928 | tf_op jit(solution)/shard_map/reduce_scatter | solution.py:300
  1200.8 160.3 %reduce-scatter.18.cloned.1.call-done = f32[48,2048]{1,0:T(8,128)} async-done(((f32[1536,2048]{1,0:T(8,128)}), f32[48,2048]{1,0:T(8,128)}) %reduce-scatter.18.cloned.1.call-update) | async-done | bytes 393232 | tf_op jit(solution)/shard_map/reduce_scatter | solution.py:298
  (151 shorter events, 16.2 us)
Async XLA Ops:
  7.2 75.9 %all-gather.9.cloned.1.call-start = ((), (), s32[]{:S(2)}) async-start(), calls=%async_computation.9 | async-start | bytes 6488064 | tf_op jit(solution)/shard_map/all_gather | solution.py:81
  7.9 140.3 %all-gather.11.cloned.1.call-start = ((), (), s32[]{:S(2)}) async-start(), calls=%async_computation.10 | async-start | bytes 4866048 | tf_op jit(solution)/shard_map/all_gather | solution.py:83
  8.7 248.4 %all-gather.15.cloned.1.call-start = ((), (), s32[]{:S(2)}) async-start(), calls=%async_computation.12 | async-start | bytes 7962624 | tf_op jit(solution)/shard_map/all_gather | solution.py:88
  9.4 267.4 %all-gather.13.cloned.1.call-start = ((), (), s32[]{:S(2)}) async-start(), calls=%async_computation.11 | async-start | bytes 1966080 | tf_op jit(solution)/shard_map/all_gather | solution.py:183
  56.5 31.0 %copy-start.12 = (f32[128,64]{1,0:T(8,128)}, f32[128,64]{1,0:T(8,128)S(1)}, u32[]{:S(2)}) copy-start(f32[128,64]{1,0:T(8,128)S(1)} %get-tuple-element.136) | copy-start | bytes 98308
  56.5 31.0 %copy-start.14 = (f32[128,64]{1,0:T(8,128)}, f32[128,64]{1,0:T(8,128)S(1)}, u32[]{:S(2)}) copy-start(f32[128,64]{1,0:T(8,128)S(1)} %get-tuple-element.137) | copy-start | bytes 98308
  56.6 31.5 %copy-start.17 = (f32[128,64]{0,1:T(8,128)}, f32[128,64]{0,1:T(8,128)S(1)}, u32[]{:S(2)}) copy-start(f32[128,64]{0,1:T(8,128)S(1)} %copy.113) | copy-start | bytes 98308
  56.7 31.4 %copy-start.19 = (f32[128,64]{0,1:T(8,128)}, f32[128,64]{0,1:T(8,128)S(1)}, u32[]{:S(2)}) copy-start(f32[128,64]{0,1:T(8,128)S(1)} %copy.114) | copy-start | bytes 98308
  57.9 25.2 %copy-start.28 = (f32[128]{0:T(128)}, f32[128]{0:T(128)S(1)}, u32[]{:S(2)}) copy-start(f32[128]{0:T(128)S(1)} %fusion.23) | copy-start | bytes 1540
  58.0 25.1 %copy-start.23 = (f32[128]{0:T(128)}, f32[128]{0:T(128)S(1)}, u32[]{:S(2)}) copy-start(f32[128]{0:T(128)S(1)} %fusion.36) | copy-start | bytes 1540
  88.4 15.5 %copy-start.6 = (bf16[128,12,64]{2,0,1:T(8,128)(2,1)}, bf16[128,12,64]{2,0,1:T(8,128)(2,1)S(1)}, u32[]{:S(2)}) copy-start(bf16[128,12,64]{2,0,1:T(8,128)(2,1)S(1)} %copy.115) | copy-start | bytes 589828
  102.0 2.0 copy-start.9
  102.0 4.2 copy-start.16
  102.0 4.2 copy-start.21
  105.5 42.6 %copy-start.3 = (bf16[1,128,1536]{2,1,0:T(8,128)(2,1)S(1)}, bf16[1,128,1536]{2,1,0:T(8,128)(2,1)}, u32[]{:S(2)}) copy-start(bf16[1,128,1536]{2,1,0:T(8,128)(2,1)} %param.11) | copy-start | bytes 1179652
  105.6 0.6 copy-start.25
  152.4 0.5 copy-start.30
  152.4 0.9 copy-start
  152.9 0.5 copy-start.27
  154.3 232.9 %all-gather.17.cloned.1.call-start = ((), (), s32[]{:S(2)}) async-start(), calls=%async_computation.13 | async-start | bytes 7962624 | tf_op jit(solution)/shard_map/all_gather | solution.py:89
  154.9 251.5 %all-gather.21.cloned.1.call-start = ((), (), s32[]{:S(2)}) async-start(), calls=%async_computation.22 | async-start | bytes 1966080 | tf_op jit(solution)/shard_map/all_gather | solution.py:202
  155.5 361.5 %all-gather.19.cloned.1.call-start = ((), (), s32[]{:S(2)}) async-start(), calls=%async_computation.14 | async-start | bytes 7962624 | tf_op jit(solution)/shard_map/all_gather | solution.py:90
  156.3 413.3 %reduce-scatter.16.cloned.1.call-start = ((), (), s32[]{:S(2)}) async-start(), calls=%async_computation.16 | async-start | bytes 1966080 | tf_op jit(solution)/shard_map/reduce_scatter | solution.py:211
  530.3 7.8 copy-start.35
  530.3 7.9 copy-start.34
  530.3 7.9 copy-start.31
  543.2 57.6 %reduce-scatter.14.cloned.1.call-start = ((), (), s32[]{:S(2)}) async-start(), calls=%async_computation.15 | async-start | bytes 1966080 | tf_op jit(solution)/shard_map/reduce_scatter | solution.py:189
  552.0 105.9 %reduce-scatter.28.cloned.1.call-start = ((), (), s32[]{:S(2)}) async-start(), calls=%async_computation.23 | async-start | bytes 327680
  603.3 0.9 copy-start.1
  604.2 7.1 copy-start.26
  611.3 3.5 copy-start.7
  611.4 3.5 copy-start.8
  613.7 1.1 copy-start.4
  618.2 43.4 %reduce-scatter.30.cloned.1.call-start = ((), (), s32[]{:S(2)}) async-start(), calls=%async_computation.24 | async-start | bytes 327680
  622.7 172.6 %reduce-scatter.22.cloned.1.call-start = ((), (), s32[]{:S(2)}) async-start(), calls=%async_computation.19 | async-start | bytes 7962624 | tf_op jit(solution)/shard_map/reduce_scatter | solution.py:305
  631.7 1.4 copy-start.32
  631.7 295.6 %reduce-scatter.24.cloned.1.call-start = ((), (), s32[]{:S(2)}) async-start(), calls=%async_computation.20 | async-start | bytes 7962624 | tf_op jit(solution)/shard_map/reduce_scatter | solution.py:308
  640.6 1.4 copy-start.33
  640.7 418.5 %reduce-scatter.26.cloned.1.call-start = ((), (), s32[]{:S(2)}) async-start(), calls=%async_computation.21 | async-start | bytes 7962624 | tf_op jit(solution)/shard_map/reduce_scatter | solution.py:311
  649.6 1.1 copy-start.2
  649.6 1.2 copy-start.11
  649.6 551.1 %reduce-scatter.20.cloned.1.call-start = ((), (), s32[]{:S(2)}) async-start(), calls=%async_computation.18 | async-start | bytes 9732096 | tf_op jit(solution)/shard_map/reduce_scatter | solution.py:300
  655.9 1.4 copy-start.5
  655.9 1.5 copy-start.10
  655.9 1.8 copy-start.18
  655.9 1.9 copy-start.20
  655.9 3.2 copy-start.13
  655.9 3.2 copy-start.15
  655.9 6.6 copy-start.24
  655.9 705.1 %reduce-scatter.18.cloned.1.call-start = ((), (), s32[]{:S(2)}) async-start(), calls=%async_computation.17 | async-start | bytes 12976128 | tf_op jit(solution)/shard_map/reduce_scatter | solution.py:298
  669.2 5.1 copy-start.22
  669.2 50.0 %copy-start.29 = (f32[128]{0:T(128)S(1)}, f32[128]{0:T(128)}, u32[]{:S(2)}) copy-start(f32[128]{0:T(128)} %copy-done.28) | copy-start | bytes 1540
Sparse Core Ops, SparseCore 0:
  10.8 72.2 all-gather.8
  86.0 62.1 all-gather.10
  150.4 106.5 all-gather.14
  259.0 17.7 all-gather.12
  278.9 108.2 all-gather.16
  388.6 17.7 all-gather.20
  408.6 108.2 all-gather.18
  543.3 26.2 reduce-scatter.15
  572.7 28.0 reduce-scatter.13
  618.3 20.0 reduce-scatter.27
  641.4 20.0 reduce-scatter.29
  665.1 130.1 reduce-scatter.21
  799.0 128.2 reduce-scatter.23
  930.8 128.2 reduce-scatter.25
  1065.4 135.2 reduce-scatter.19
  1207.2 153.7 reduce-scatter.17
where the time goes:
time: 1380 us; the launch traced here: 1370 us
  waiting for transfers between devices  1090 us (79%)
  matrix products  117 us (8%)
  blocking collectives  97.3 us (7%)
  local copies, waits for them, and re-layouts  23.7 us (2%)
  other arithmetic  23 us (2%)
  between operations  14.7 us (1%)
    reduce_scatter x1, waiting for transfers between devices, shards(): lax.psum_scatter(grad_wqkv, ('wide', 'narrow'), scatter_dimension=0, tile...  160 us
    reduce_scatter x1, waiting for transfers between devices, shards(): lax.psum_scatter(grad_wout, ('wide', 'narrow'), scatter_dimension=1, tile...  139 us
    reduce_scatter x1, waiting for transfers between devices, shards(): lax.psum_scatter(grad_wup.astype(jnp.bfloat16), 'wide', scatter_dimension...  130 us
    reduce_scatter x1, waiting for transfers between devices, shards(): lax.psum_scatter(grad_wdown.astype(jnp.bfloat16), 'wide', scatter_dimensi...  129 us
    all_gather x1, waiting for transfers between devices, shards(): lax.all_gather(w_down, 'wide', axis=1, tiled=True)  111 us
    all_gather x1, waiting for transfers between devices, shards(): lax.all_gather(w_up, 'wide', axis=0, tiled=True)  101 us
    all_gather x1, waiting for transfers between devices, shards(): lax.all_gather(w_gate, 'wide', axis=0, tiled=True)  101 us
    unnamed x2, blocking collectives  85.6 us
  transfers between devices with their start and end apart: 16, of which 15 were waited for; matrix products, arithmetic and copies ran while one was open for 8% of the time, Pallas kernels for 0%

commit v1 on v0

--- a/solution.py
+++ b/solution.py
@@ -80,7 +80,12 @@
     wqkv_full, bias_full, wout_full, gain_one, gain_two = (
         lax.all_gather(w_qkv, ("wide", "narrow"), axis=0, tiled=True),
         lax.all_gather(b_qkv, ("wide", "narrow"), axis=0, tiled=True),
-        lax.all_gather(w_out, ("wide", "narrow"), axis=1, tiled=True),
+        jnp.concatenate(
+            lax.all_to_all(
+                jnp.stack([w_out] * lax.axis_size(("wide", "narrow"))), ("wide", "narrow"), 0, 0
+            ),
+            axis=1,
+        ),
         lax.all_gather(norm1_gain, ("wide", "narrow"), axis=0, tiled=True),
         lax.all_gather(norm2_gain, ("wide", "narrow"), axis=0, tiled=True),
     )

time: 1380 us -> 1370 us (level)
  waiting for transfers between devices: 1090 us -> 941 us
  blocking collectives: 97.3 us -> 233 us
    unnamed x2, blocking collectives: 85.6 us -> 221 us
    all_gather x1, waiting for transfers between devices: 101 us -> 15.7 us  [shards(): lax.all_gather(w_gate, 'wide', axis=0, tiled=True)]
    all_gather x1 -> x0, waiting for transfers between devices: 40.1 us -> none  [shards(): lax.all_gather(w_out, ('wide', 'narrow'), axis=1, tiled=True)]
    all_gather x1, waiting for transfers between devices: 24.4 us -> 0.01 us  [shards(): lax.all_gather(w_qkv, ('wide', 'narrow'), axis=0, tiled=True)]
  transfers between devices with their start and end apart: 16 -> 16, of which waited for: 15 -> 13; matrix products, arithmetic and copies ran while one was open for 8% -> 8% of each run, Pallas kernels for 0% -> 0%
where the time goes in v1:
time: 1370 us; the launch traced here: 1360 us
  waiting for transfers between devices  941 us (69%)
  blocking collectives  233 us (17%)
  matrix products  117 us (9%)
  local copies, waits for them, and re-layouts  27 us (2%)
  other arithmetic  20.7 us (2%)
  between operations  14.7 us (1%)
    unnamed x2, blocking collectives  221 us
    reduce_scatter x1, waiting for transfers between devices, shards(): lax.psum_scatter(grad_wqkv, ('wide', 'narrow'), scatter_dimension=0, tile...  160 us
    reduce_scatter x1, waiting for transfers between devices, shards(): lax.psum_scatter(grad_wout, ('wide', 'narrow'), scatter_dimension=1, tile...  139 us
    reduce_scatter x1, waiting for transfers between devices, shards(): lax.psum_scatter(grad_wdown.astype(jnp.bfloat16), 'wide', scatter_dimensi...  130 us
    reduce_scatter x1, waiting for transfers between devices, shards(): lax.psum_scatter(grad_wup.astype(jnp.bfloat16), 'wide', scatter_dimension...  129 us
    all_gather x1, waiting for transfers between devices, shards(): lax.all_gather(w_down, 'wide', axis=1, tiled=True)  110 us
    all_gather x1, waiting for transfers between devices, shards(): lax.all_gather(w_up, 'wide', axis=0, tiled=True)  101 us
    reduce_scatter x1, waiting for transfers between devices, shards(): lax.psum_scatter(grad_wgate.astype(jnp.bfloat16), 'wide', scatter_dimensi...  75.3 us
  transfers between devices with their start and end apart: 16, of which 13 were waited for; matrix products, arithmetic and copies ran while one was open for 8% of the time, Pallas kernels for 0%

profile of v1, /device:TPU:0, one launch (start us, length us, event | category | flops | bytes accessed | tf_op | source)
XLA Modules:
  0.0 1362.1 jit_solution(402545587067789494)
XLA Ops:
  8.7 3.6 stack.2
  12.3 7.4 all-to-all-start
  20.6 177.8 %all-reduce.11 = (bf16[2048]{0:T(1024)(128)(2,1)S(1)}, bf16[1536]{0:T(1024)(128)(2,1)S(1)}, bf16[1536]{0:T(1024)(128)(2,1)S(1)}) all-reduce(bf16[2048]{0:T(1024)(128)(2,1)S(1)} %dynamic-update-slice.1, bf16[1536]{0:T(1024)(128)(2,1)S(1)} %dynamic-update-slice, ...), channel_id=1, replica_groups=mesh['wide'=8,'narrow'=4] {'wide','narrow'}, use_global_device_ids=true, to_apply=%add.5 | all-reduce | flops 5120 | bytes 20480
  199.6 0.8 fusion.27
  200.3 3.9 convolution_add_fusion.2
  205.3 0.9 copy.116
  206.3 0.9 copy.117
  207.2 6.5 all_gather.40
  213.8 0.9 copy.133
  214.6 5.9 all_gather.39
  221.3 2.0 fusion.5
  223.2 1.6 select_reduce_fusion
  225.5 1.9 fusion.46
  227.4 4.2 multiply_reduce_fusion
  232.6 0.9 multiply_convert_fusion.3
  235.5 15.7 %all-gather.12.cloned.1.call-done = bf16[1536,2240]{1,0:T(8,128)(2,1)} async-done(((bf16[192,2240]{1,0:T(8,128)(2,1)}), bf16[1536,2240]{1,0:T(8,128)(2,1)}) %all-gather.12.cloned.1.call-update) | async-done | bytes 6881296 | tf_op jit(solution)/shard_map/all_gather | solution.py:93
  251.2 20.0 %all-gather.10.cloned.1.call-done = bf16[512,1536]{1,0:T(8,128)(2,1)} async-done(((bf16[128,1536]{1,0:T(8,128)(2,1)}), bf16[512,1536]{1,0:T(8,128)(2,1)}) %all-gather.10.cloned.1.call-update) | async-done | bytes 1572880 | tf_op jit(solution)/shard_map/all_gather | solution.py:188
  271.2 9.5 fusion.47
  280.7 100.9 %all-gather.14.cloned.1.call-done = bf16[1536,2240]{1,0:T(8,128)(2,1)} async-done(((bf16[192,2240]{1,0:T(8,128)(2,1)}), bf16[1536,2240]{1,0:T(8,128)(2,1)}) %all-gather.14.cloned.1.call-update) | async-done | bytes 6881296 | tf_op jit(solution)/shard_map/all_gather | solution.py:94
  381.6 9.3 fusion.48
  390.9 9.9 all-gather.18.cloned.1.call-done
  400.8 110.4 %all-gather.16.cloned.1.call-done = bf16[2240,1536]{0,1:T(8,128)(2,1)} async-done(((bf16[2240,192]{0,1:T(8,128)(2,1)}), bf16[2240,1536]{0,1:T(8,128)(2,1)}) %all-gather.16.cloned.1.call-update) | async-done | bytes 6881296 | tf_op jit(solution)/shard_map/all_gather | solution.py:95
  511.2 13.3 multiply_convert_fusion
  524.5 7.8 fusion.49
  532.4 5.0 fusion.3
  537.5 8.8 convolution_convert_fusion.3
  546.7 17.1 %reduce-scatter.16.cloned.1.call-done = bf16[128,1536]{1,0:T(8,128)(2,1)} async-done(((bf16[512,1536]{1,0:T(8,128)(2,1)}), bf16[128,1536]{1,0:T(8,128)(2,1)}) %reduce-scatter.16.cloned.1.call-update) | async-done | bytes 393232 | tf_op jit(solution)/shard_map/reduce_scatter | solution.py:216
  563.8 2.1 fusion.19
  565.9 1.2 multiply_multiply_fusion.1
  567.1 27.9 %reduce-scatter.14.cloned.1.call-done = bf16[128,1536]{1,0:T(8,128)(2,1)} async-done(((bf16[512,1536]{1,0:T(8,128)(2,1)}), bf16[128,1536]{1,0:T(8,128)(2,1)}) %reduce-scatter.14.cloned.1.call-update) | async-done | bytes 393232 | tf_op jit(solution)/shard_map/reduce_scatter | solution.py:194
  595.0 2.5 fusion.20
  597.5 0.9 copy-done.1
  598.4 3.9 convolution_convert_fusion.4
  602.3 1.9 copy.121
  604.2 1.3 fusion.25
  605.6 2.3 fusion.2
  607.9 1.1 copy-done.4
  609.1 1.5 fusion.10
  610.6 1.8 copy.156
  612.4 2.6 fusion.11
  615.1 1.8 copy.158
  616.9 8.9 convolution_convert_fusion.2
  626.0 1.3 copy-done.31
  627.3 7.6 convolution_convert_fusion.1
  635.1 1.2 copy-done.32
  636.3 7.5 convolution_convert_fusion
  643.9 1.1 copy-done.2
  645.1 5.0 fusion.28
  650.2 1.3 copy-done.5
  652.2 0.9 copy.157
  653.6 1.9 reduce-scatter.30.cloned.1.call-done
  655.6 0.9 copy.159
  656.6 6.4 fusion.31
  663.2 5.1 fusion.17
  668.4 43.0 %all-reduce.10 = (f32[2048]{0:T(1024)S(1)}, f32[1536]{0:T(1024)S(1)}, f32[1536]{0:T(1024)S(1)}) all-reduce(f32[2048]{0:T(1024)S(1)} %convert_reduce_fusion, f32[1536]{0:T(1024)S(1)} %get-tuple-element.83, f32[1536]{0:T(1024)S(1)} %copy-done.21), channel_id=8, replica_groups=mesh['wide'=8,'narrow'=4] {'wide','narrow'}, use_global_device_ids=true, to_apply=%region_16.17.clone | all-reduce | flops 5120 | bytes 40960
  713.1 1.1 fusion.22
  714.3 75.3 %reduce-scatter.22.cloned.1.call-done = bf16[192,2240]{1,0:T(8,128)(2,1)} async-done(((bf16[1536,2240]{1,0:T(8,128)(2,1)}), bf16[192,2240]{1,0:T(8,128)(2,1)}) %reduce-scatter.22.cloned.1.call-update) | async-done | bytes 860176 | tf_op jit(solution)/shard_map/reduce_scatter | solution.py:310
  789.5 2.5 convert_element_type.174
  792.0 129.4 %reduce-scatter.24.cloned.1.call-done = bf16[192,2240]{1,0:T(8,128)(2,1)} async-done(((bf16[1536,2240]{1,0:T(8,128)(2,1)}), bf16[192,2240]{1,0:T(8,128)(2,1)}) %reduce-scatter.24.cloned.1.call-update) | async-done | bytes 860176 | tf_op jit(solution)/shard_map/reduce_scatter | solution.py:313
  921.4 2.5 convert_element_type.176
  923.9 129.5 %reduce-scatter.26.cloned.1.call-done = bf16[2240,192]{0,1:T(8,128)(2,1)} async-done(((bf16[2240,1536]{0,1:T(8,128)(2,1)}), bf16[2240,192]{0,1:T(8,128)(2,1)}) %reduce-scatter.26.cloned.1.call-update) | async-done | bytes 860176 | tf_op jit(solution)/shard_map/reduce_scatter | solution.py:316
  1053.4 2.5 convert_element_type.178
  1055.9 139.2 %reduce-scatter.20.cloned.1.call-done = f32[1536,48]{0,1:T(8,128)} async-done(((f32[1536,1536]{0,1:T(8,128)}), f32[1536,48]{0,1:T(8,128)}) %reduce-scatter.20.cloned.1.call-update) | async-done | bytes 294928 | tf_op jit(solution)/shard_map/reduce_scatter | solution.py:305
  1195.1 160.3 %reduce-scatter.18.cloned.1.call-done = f32[48,2048]{1,0:T(8,128)} async-done(((f32[1536,2048]{1,0:T(8,128)}), f32[48,2048]{1,0:T(8,128)}) %reduce-scatter.18.cloned.1.call-update) | async-done | bytes 393232 | tf_op jit(solution)/shard_map/reduce_scatter | solution.py:303
  (157 shorter events, 13.0 us)
Async XLA Ops:
  7.2 193.1 %all-gather.8.cloned.1.call-start = ((), (), s32[]{:S(2)}) async-start(), calls=%async_computation.10 | async-start | bytes 6488064 | tf_op jit(solution)/shard_map/all_gather | solution.py:81
  7.9 243.3 %all-gather.12.cloned.1.call-start = ((), (), s32[]{:S(2)}) async-start(), calls=%async_computation.12 | async-start | bytes 7962624 | tf_op jit(solution)/shard_map/all_gather | solution.py:93
  12.3 7.5 copy-start.33
  12.3 7.8 copy-start.34
  12.3 8.1 copy-start.35
  12.3 186.1 %copy-start.36 = (s32[1,8]{1,0:T(1,128)S(1)}, s32[1,8]{1,0:T(1,128)}, u32[]{:S(2)}) copy-start(s32[1,8]{1,0:T(1,128)} %param.12) | copy-start | bytes 100
  12.3 187.1 %copy-start.3 = (bf16[1,128,1536]{2,1,0:T(8,128)(2,1)S(1)}, bf16[1,128,1536]{2,1,0:T(8,128)(2,1)}, u32[]{:S(2)}) copy-start(bf16[1,128,1536]{2,1,0:T(8,128)(2,1)} %param.11) | copy-start | bytes 1179652
  12.3 215.1 %all-to-all-start = ((bf16[32,1536,48]{1,2,0:T(8,128)(2,1)}), bf16[32,1536,48]{1,2,0:T(8,128)(2,1)}, u32[]{:S(2)}, u32[]{:S(2)}) async-start(bf16[32,1536,48]{1,2,0:T(8,128)(2,1)} %stack.2), calls=%async_computation | async-start | bytes 9437184 | tf_op jit(solution)/shard_map/all_to_all | solution.py:84
  19.7 251.5 %all-gather.10.cloned.1.call-start = ((), (), s32[]{:S(2)}) async-start(), calls=%async_computation.11 | async-start | bytes 1966080 | tf_op jit(solution)/shard_map/all_gather | solution.py:188
  199.1 5.6 copy-start.11
  199.1 5.6 copy-start.13
  199.2 6.0 copy-start.16
  199.2 6.0 copy-start.18
  199.5 0.8 copy-start.27
  199.5 0.8 copy-start.22
  220.5 0.7 copy-start.8
  221.2 4.2 copy-start.15
  221.2 4.2 copy-start.20
  224.9 0.6 copy-start.24
  231.6 0.5 copy-start.29
  231.6 0.9 copy-start
  232.1 0.5 copy-start.26
  233.5 148.1 %all-gather.14.cloned.1.call-start = ((), (), s32[]{:S(2)}) async-start(), calls=%async_computation.13 | async-start | bytes 7962624 | tf_op jit(solution)/shard_map/all_gather | solution.py:94
  234.1 166.7 %all-gather.18.cloned.1.call-start = ((), (), s32[]{:S(2)}) async-start(), calls=%async_computation.22 | async-start | bytes 1966080 | tf_op jit(solution)/shard_map/all_gather | solution.py:207
  234.7 276.5 %all-gather.16.cloned.1.call-start = ((), (), s32[]{:S(2)}) async-start(), calls=%async_computation.14 | async-start | bytes 7962624 | tf_op jit(solution)/shard_map/all_gather | solution.py:95
  235.3 328.5 %reduce-scatter.16.cloned.1.call-start = ((), (), s32[]{:S(2)}) async-start(), calls=%async_computation.16 | async-start | bytes 1966080 | tf_op jit(solution)/shard_map/reduce_scatter | solution.py:216
  524.5 7.8 copy-start.38
  524.5 7.9 copy-start.37
  524.5 7.9 copy-start.30
  537.4 57.6 %reduce-scatter.14.cloned.1.call-start = ((), (), s32[]{:S(2)}) async-start(), calls=%async_computation.15 | async-start | bytes 1966080 | tf_op jit(solution)/shard_map/reduce_scatter | solution.py:194
  546.3 105.9 %reduce-scatter.28.cloned.1.call-start = ((), (), s32[]{:S(2)}) async-start(), calls=%async_computation.23 | async-start | bytes 327680
  597.5 0.9 copy-start.1
  598.4 7.1 copy-start.25
  605.6 3.5 copy-start.6
  605.6 3.5 copy-start.7
  607.9 1.1 copy-start.4
  612.4 43.2 %reduce-scatter.30.cloned.1.call-start = ((), (), s32[]{:S(2)}) async-start(), calls=%async_computation.24 | async-start | bytes 327680
  616.9 172.6 %reduce-scatter.22.cloned.1.call-start = ((), (), s32[]{:S(2)}) async-start(), calls=%async_computation.19 | async-start | bytes 7962624 | tf_op jit(solution)/shard_map/reduce_scatter | solution.py:310
  625.9 1.4 copy-start.31
  625.9 295.5 %reduce-scatter.24.cloned.1.call-start = ((), (), s32[]{:S(2)}) async-start(), calls=%async_computation.20 | async-start | bytes 7962624 | tf_op jit(solution)/shard_map/reduce_scatter | solution.py:313
  634.9 1.4 copy-start.32
  634.9 418.5 %reduce-scatter.26.cloned.1.call-start = ((), (), s32[]{:S(2)}) async-start(), calls=%async_computation.21 | async-start | bytes 7962624 | tf_op jit(solution)/shard_map/reduce_scatter | solution.py:316
  643.8 1.1 copy-start.2
  643.8 1.2 copy-start.10
  643.9 551.2 %reduce-scatter.20.cloned.1.call-start = ((), (), s32[]{:S(2)}) async-start(), calls=%async_computation.18 | async-start | bytes 9732096 | tf_op jit(solution)/shard_map/reduce_scatter | solution.py:305
  650.1 1.4 copy-start.5
  650.1 1.5 copy-start.9
  650.1 1.9 copy-start.17
  650.1 1.9 copy-start.19
  650.1 3.2 copy-start.12
  650.1 3.2 copy-start.14
  650.1 6.4 copy-start.23
  650.1 705.2 %reduce-scatter.18.cloned.1.call-start = ((), (), s32[]{:S(2)}) async-start(), calls=%async_computation.17 | async-start | bytes 12976128 | tf_op jit(solution)/shard_map/reduce_scatter | solution.py:303
  663.2 5.1 copy-start.21
  663.2 49.9 %copy-start.28 = (f32[128]{0:T(128)S(1)}, f32[128]{0:T(128)}, u32[]{:S(2)}) copy-start(f32[128]{0:T(128)} %copy-done.27) | copy-start | bytes 1540
Sparse Core Ops, SparseCore 0:
  10.8 123.2 all-gather.7
  136.4 114.8 all-gather.11
  253.4 17.7 all-gather.9
  273.3 108.2 all-gather.13
  383.0 17.7 all-gather.17
  402.9 108.2 all-gather.15
  537.6 26.2 reduce-scatter.15
  566.9 28.0 reduce-scatter.13
  612.5 20.0 reduce-scatter.27
  635.5 20.0 reduce-scatter.29
  659.3 130.2 reduce-scatter.21
  793.1 128.2 reduce-scatter.23
  925.1 128.2 reduce-scatter.25
  1059.8 135.2 reduce-scatter.19
  1201.5 153.7 reduce-scatter.17
